TPU v7x, 32 devices: a whole 2x2x4 slice. The times are simulated.
32 devices in a mesh: lat: 8 (over y, x, core), lon: 4 (over z).
Axes of the slice: x: 2, y: 2, z: 4, core: 2. Of those that a mesh axis runs over, the one named last changes fastest.
Arguments:
- loadings: float32 [176, 720, 200], P('lat', 'lon'), may hold values from -60 to 60, as said below
Outputs:
- rotated: float32 [176, 720, 200], P('lat', 'lon')
- rotation: float32 [200, 200], replicated
Inputs may be any that keep to these rules, and one draw needn't show every extreme that they name: Every grid point's loadings are not all zero.
All inputs are finite; a program needn't handle non-finite values.
Results may differ from a plain program's by a relative error of at most 0.00011.
Values sent between devices are 32-bit elements; how exact they have to be, the bound alone decides.
No kernel may reach another device: no remote copies, remote signals or barrier semaphores. Data moves between devices by JAX's collectives and lax.ppermute only.
A program may use at most 64 MiB of HBM per device.

v0:
```python
import math

import jax
import jax.numpy as jnp
from jax import lax
from jax.sharding import PartitionSpec as P

SWEEPS = 2
NS_STEPS = 20


def matmul(left, right):
    return jnp.dot(left, right, precision=lax.Precision.HIGHEST)


def polar_factor(gradient, count_steps):
    iterate = gradient / jnp.sqrt(jnp.sum(gradient * gradient))
    for count in range(count_steps):
        iterate = 1.5 * iterate - 0.5 * matmul(iterate, matmul(iterate.T, iterate))
    return iterate


def latitude_weight(rows, lat_total):
    degrees = -90.0 + (rows.astype(jnp.float32) + 0.5) * (180.0 / lat_total)
    return jnp.cos(degrees * (math.pi / 180.0))


def reduce_pair(cubic, colsq):
    return lax.psum((cubic, colsq), ("lat", "lon"))


def shards(loadings):
    lat_rows, lon_cols, modes = loadings.shape
    lat_total = lat_rows * lax.axis_size("lat")
    lon_total = lon_cols * lax.axis_size("lon")
    row_norm = jnp.sqrt(jnp.sum(loadings * loadings, axis=-1, keepdims=True) + 1e-06)
    normed = (loadings / row_norm).reshape(lat_rows * lon_cols, modes)
    own_rows = lax.axis_index("lat") * lat_rows + jnp.arange(lat_rows)
    weights = latitude_weight(own_rows, lat_total)
    weight_rows = jnp.repeat(weights, lon_cols).reshape(lat_rows * lon_cols, 1)
    total = jnp.sum(latitude_weight(jnp.arange(lat_total), lat_total)) * lon_total
    weighted = weight_rows * normed
    rotation = jnp.eye(modes, dtype=jnp.float32)
    gram = lax.psum(matmul(weighted.T, normed), ("lat", "lon"))
    for sweep_index in range(SWEEPS):
        spun = matmul(normed, rotation)
        cubic_local = matmul(weighted.T, spun * spun * spun)
        colsq_local = jnp.sum(weight_rows * spun * spun, axis=0)
        cubic, colsq = reduce_pair(cubic_local, colsq_local)
        gradient = cubic - matmul(gram, rotation) * (colsq / total)[None, :]
        rotation = polar_factor(gradient, NS_STEPS)
    rotated = matmul(normed, rotation).reshape(lat_rows, lon_cols, modes) * row_norm
    return (rotated, rotation)


def solution(mesh):
    return jax.shard_map(
        shards,
        mesh=mesh,
        in_specs=(P("lat", "lon", None),),
        out_specs=(P("lat", "lon", None), P()),
        check_vma=False,
    )
```

profile of v0, /device:TPU:0, one launch (start us, length us, event | category | flops | bytes accessed | tf_op | source)
XLA Modules:
  0.0 399.6 jit_solution(6151187368524490698)
XLA Ops:
  7.3 3.1 multiply_reduce_fusion
  10.6 2.3 broadcast_divide_fusion
  13.0 4.8 %reshape.28 = f32[3960,200]{1,0:T(8,128)} reshape(f32[22,180,200]{2,1,0:T(8,128)} %broadcast_divide_fusion) | data formatting | bytes 6336000 | tf_op jit(solution)/shard_map/reshape | solution.py:37
  17.8 11.0 %fusion.11 = f32[200,200]{1,0:T(8,128)} fusion(f32[22,180,200]{2,1,0:T(8,128)} %broadcast_divide_fusion, f32[22]{0:T(128)S(1)} %multiply_cosine_fusion), kind=kOutput, calls=%fused_computation.18 | convolution fusion | flops 1901592064 | bytes 3328088 | tf_op jit(solution)/shard_map/dot_general | solution.py:13
  29.0 3.9 copy.5
  32.9 4.8 %fusion.3 = (f32[200]{0:T(256)S(1)}, f32[3960,200]{0,1:T(8,128)S(1)}) fusion(f32[3960]{0:T(1024)S(1)} %mul.344, f32[3960,200]{1,0:T(8,128)} %reshape.28), kind=kOutput, calls=%fused_computation.8 | convolution fusion | flops 1903215872 | bytes 6352640 | tf_op jit(solution)/shard_map/dot_general | solution.py:13
  37.6 3.8 fusion.2
  41.5 0.6 cosine_reduce_fusion
  42.2 42.3 %psum.37 = f32[200]{0:T(256)S(1)} all-reduce(f32[200]{0:T(256)S(1)} %get-tuple-element.4), channel_id=1, replica_groups=mesh['lat'=8,'lon'=4] {'lat','lon'}, use_global_device_ids=true, to_apply=%region_4.0 | all-reduce | flops 200 | bytes 1600 | tf_op jit(solution)/shard_map/psum | solution.py:29
  85.0 87.1 %all-reduce.6.cloned.1.call-done = (f32[200,200]{1,0:T(8,128)}, f32[200,200]{1,0:T(8,128)}) async-done(((f32[200,200]{1,0:T(8,128)}, f32[200,200]{1,0:T(8,128)}), (f32[200,200]{1,0:T(8,128)}, f32[200,200]{1,0:T(8,128)})) %all-reduce.6.cloned.1.call-update) | async-done | bytes 320016 | tf_op jit(solution)/shard_map/psum | solution.py:29
  172.1 1.9 multiply_reduce_fusion.2
  174.7 0.5 fusion.58
  175.3 0.3 fusion.54
  175.6 0.5 fusion.60
  176.1 0.3 fusion.53
  176.5 0.5 fusion.61
  177.4 0.5 fusion.62
  178.3 0.5 fusion.63
  179.1 0.5 fusion.64
  179.7 0.3 fusion.49
  180.0 0.5 fusion.65
  180.9 0.5 fusion.66
  181.8 0.5 fusion.67
  182.7 0.5 fusion.68
  183.6 0.5 fusion.69
  184.4 0.5 fusion.70
  185.3 0.5 fusion.71
  186.2 0.5 fusion.72
  187.1 0.5 fusion.73
  188.0 0.7 fusion.74
  188.7 0.3 fusion.39
  189.0 0.5 fusion.75
  189.6 0.3 fusion.38
  189.9 0.5 fusion.76
  190.5 0.3 fusion.37
  190.8 0.5 fusion.77
  191.7 0.5 fusion.78
  192.6 4.3 %fusion.5 = (f32[200]{0:T(256)S(1)}, f32[3960,200]{0,1:T(8,128)S(1)}) fusion(f32[3960]{0:T(1024)S(1)} %mul.344, f32[3960,200]{1,0:T(8,128)S(1)} %copy-done.1, f32[200,200]{1,0:T(8,128)S(1)} %fusion.35), kind=kOutput, calls=%fused_computation.10 | convolution fusion | flops 1903175808 | bytes 6512640 | tf_op jit(solution)/shard_map/dot_general | solution.py:13
  196.9 3.8 fusion.4
  200.7 41.3 %psum.39 = f32[200]{0:T(256)S(1)} all-reduce(f32[200]{0:T(256)S(1)} %get-tuple-element.8), channel_id=1, replica_groups=mesh['lat'=8,'lon'=4] {'lat','lon'}, use_global_device_ids=true, to_apply=%region_9.0 | all-reduce | flops 200 | bytes 1600 | tf_op jit(solution)/shard_map/psum | solution.py:29
  242.0 124.8 %all-reduce.4.cloned.1.call-done = f32[200,200]{1,0:T(8,128)} async-done(((f32[200,200]{1,0:T(8,128)}), f32[200,200]{1,0:T(8,128)}) %all-reduce.4.cloned.1.call-update) | async-done | bytes 160016 | tf_op jit(solution)/shard_map/psum | solution.py:29
  366.8 2.0 multiply_reduce_fusion.1
  369.4 0.5 fusion.59
  370.0 0.3 fusion.33
  370.3 0.5 fusion.79
  371.2 0.5 fusion.80
  372.1 0.5 fusion.81
  373.0 0.5 fusion.82
  373.9 0.5 fusion.83
  374.7 0.5 fusion.84
  375.6 0.5 fusion.85
  376.5 0.5 fusion.86
  377.4 0.5 fusion.87
  378.3 0.5 fusion.88
  379.2 0.5 fusion.89
  380.1 0.5 fusion.90
  380.9 0.5 fusion.91
  381.8 0.5 fusion.92
  382.7 0.8 fusion.93
  383.9 0.5 fusion.94
  384.7 0.5 fusion.95
  385.6 0.5 fusion.96
  386.5 0.5 fusion.97
  387.4 4.9 %convolution_multiply_fusion = f32[22,180,200]{2,1,0:T(8,128)} fusion(f32[22,180,200]{2,1,0:T(8,128)S(1)} %copy-done, f32[22,180]{1,0:T(8,128)S(1)} %add_sqrt_fusion, f32[200,200]{1,0:T(8,128)S(1)} %fusion.14), kind=kOutput, calls=%fused_computation.13 | convolution fusion | flops 1901592064 | bytes 6511840 | tf_op jit(solution)/shard_map/dot_general | solution.py:13
  (51 shorter events, 11.4 us)
Async XLA Ops:
  7.2 165.0 %all-reduce.6.cloned.1.call-start = ((), (), s32[]{:S(2)}) async-start(), calls=%async_computation.1 | async-start | bytes 819200 | tf_op jit(solution)/shard_map/psum | solution.py:29
  7.2 3.4 copy-start.2
  41.5 325.3 %all-reduce.4.cloned.1.call-start = ((), (), s32[]{:S(2)}) async-start(), calls=%async_computation | async-start | bytes 409600 | tf_op jit(solution)/shard_map/psum | solution.py:29
  188.0 4.6 %copy-start.1 = (f32[3960,200]{1,0:T(8,128)S(1)}, f32[3960,200]{1,0:T(8,128)}, u32[]{:S(2)}) copy-start(f32[3960,200]{1,0:T(8,128)} %reshape.28) | copy-start | bytes 9504004
  382.7 4.7 %copy-start = (f32[22,180,200]{2,1,0:T(8,128)S(1)}, f32[22,180,200]{2,1,0:T(8,128)}, u32[]{:S(2)}) copy-start(f32[22,180,200]{2,1,0:T(8,128)} %broadcast_divide_fusion) | copy-start | bytes 9504004
  387.4 4.9 %copy-start.3 = (f32[200,200]{1,0:T(8,128)}, f32[200,200]{1,0:T(8,128)S(1)}, u32[]{:S(2)}) copy-start(f32[200,200]{1,0:T(8,128)S(1)} %fusion.14) | copy-start | bytes 480004
Sparse Core Ops, SparseCore 0:
  41.6 130.4 all-reduce.5
  242.1 124.6 all-reduce.3
where the time goes:
time: 407 us; the launch traced here: 400 us
  waiting for transfers between devices  212 us (52%)
  blocking collectives  83.5 us (21%)
  matrix products  71.6 us (18%)
  between operations  17.2 us (4%)
  local copies, waits for them, and re-layouts  9.12 us (2%)
  other arithmetic  6.21 us (2%)
    psum x2, waiting for transfers between devices, reduce_pair(): return lax.psum((cubic, colsq), ('lat', 'lon'))  212 us
    psum x2, blocking collectives, reduce_pair(): return lax.psum((cubic, colsq), ('lat', 'lon'))  83.5 us
    dot_general x88, matrix products, matmul(): return jnp.dot(left, right, precision=lax.Precision.HIGHEST)  71.6 us
    reshape x2, local copies, waits for them, and re-layouts, shards(): normed = (loadings / row_norm).reshape(lat_rows * lon_cols, modes)  8.73 us
  transfers between devices with their start and end apart: 2, of which 2 were waited for; matrix products, arithmetic and copies ran while one was open for 0% of the time, Pallas kernels for 0%

commit v1 on v0

v1 whole, which is shorter than its diff:
```python
import functools
import math

import jax
import jax.numpy as jnp
from jax import lax
from jax.experimental import pallas as pl
from jax.experimental.pallas import tpu as pltpu
from jax.sharding import PartitionSpec as P

SWEEPS = 2
NS_STEPS = 20
AXES = ("lat", "lon")
F32 = jnp.float32
BF16 = jnp.bfloat16


def latitude_weight(rows, lat_total):
    degrees = -90.0 + (rows.astype(jnp.float32) + 0.5) * (180.0 / lat_total)
    return jnp.cos(degrees * (math.pi / 180.0))


def halves(value):
    high = value.astype(BF16)
    return high, (value - high.astype(F32)).astype(BF16)


def dot_nn(left, right):
    return lax.dot_general(left, right, (((1,), (0,)), ((), ())), preferred_element_type=F32)


def dot_nt(left, right):
    return lax.dot_general(left, right, (((1,), (1,)), ((), ())), preferred_element_type=F32)


def triple(dot, left, right):
    return dot(left[0], right[0]) + (dot(left[0], right[1]) + dot(left[1], right[0]))


def polar_transposed(gradient):
    iterate = gradient / jnp.sqrt(jnp.sum(gradient * gradient))

    def step(_, current):
        parts = halves(current)
        inner = triple(dot_nt, parts, parts)
        return 1.5 * current - 0.5 * triple(dot_nn, halves(inner), parts)

    return lax.fori_loop(0, NS_STEPS, step, iterate)


def group_of(lat_rows):
    return max(d for d in range(1, min(lat_rows, 11) + 1) if lat_rows % d == 0)


def normalize_rows(x_ref, first, count, stage):
    cols = x_ref.shape[1]
    pad = stage.shape[0] // count
    for r in range(count):
        x = x_ref[first + r]
        norm = jnp.sqrt(jnp.sum(x * x, axis=-1, keepdims=True) + 1e-06)
        stage[r * pad:r * pad + cols, :] = x * (1.0 / norm)


def products(left, parts):
    return triple(dot_nn, halves(left), parts)


def first_kernel(x_ref, w_ref, out_ref, stage, *, count):
    step = pl.program_id(0)

    @pl.when(step == 0)
    def _():
        stage[...] = jnp.zeros_like(stage)
        out_ref[...] = jnp.zeros_like(out_ref)

    normalize_rows(x_ref, 0, count, stage)
    normed = stage[...]
    parts = halves(normed)
    flipped = normed.T
    weighted = flipped * w_ref[0]
    modes = normed.shape[1]
    out_ref[0, 0:modes, :] += products(weighted, parts)
    out_ref[1, 0:modes, :] += products(weighted * flipped * flipped, parts)


def diagonal(square):
    rows = lax.broadcasted_iota(jnp.int32, square.shape, 0)
    cols = lax.broadcasted_iota(jnp.int32, square.shape, 1)
    return jnp.sum(jnp.where(rows == cols, square, 0.0), axis=1, keepdims=True)


def middle_kernel(total_ref, sums_ref, w_ref, x_hbm, out_ref, rot_ref, x_ref, stage, sem, *, count):
    copy = pltpu.make_async_copy(x_hbm, x_ref, sem)
    copy.start()
    modes = x_ref.shape[2]
    gram = sums_ref[0, 0:modes, :]
    cubic = sums_ref[1, 0:modes, :]
    rotation = polar_transposed(cubic - gram * (diagonal(gram) / total_ref[0]))
    rot_ref[...] = rotation
    stage[...] = jnp.zeros_like(stage)
    out_ref[...] = jnp.zeros_like(out_ref)
    copy.wait()
    rot_parts = halves(rotation)

    def body(step, _):
        normalize_rows(x_ref, step * count, count, stage)
        parts = halves(stage[...])
        spun = triple(dot_nt, rot_parts, parts)
        cubed = spun * spun * spun * w_ref[step]
        out_ref[0:modes, :] += products(cubed, parts)
        return 0

    lax.fori_loop(0, x_ref.shape[0] // count, body, 0)


def last_kernel(total_ref, gram_ref, old_ref, cubic_ref, x_hbm, out_hbm, rot_ref, x_ref, out_ref, sem, sems):
    copy = pltpu.make_async_copy(x_hbm, x_ref, sem)
    copy.start()
    lat_rows, _, modes = x_ref.shape
    old = old_ref[...]
    turned = triple(dot_nn, halves(old), halves(gram_ref[0, 0:modes, :]))
    colsq = jnp.sum(turned * old, axis=1, keepdims=True)
    rotation = polar_transposed(cubic_ref[0:modes, :] - turned * (colsq / total_ref[0]))
    rot_ref[...] = rotation.T
    parts = halves(rotation)
    copy.wait()
    writes = []
    for r in range(lat_rows):
        out_ref[r] = triple(dot_nt, halves(x_ref[r]), parts)
        write = pltpu.make_async_copy(out_ref.at[r], out_hbm.at[r], sems.at[r])
        write.start()
        writes.append(write)
    for write in writes:
        write.wait()


def exchange_sum(value):
    lon = lax.axis_size("lon")
    lat = lax.axis_size("lat")
    devices = lat * lon

    def send(data, lat_mask, lon_mask):
        pairs = [(i, ((i // lon) ^ lat_mask) * lon + ((i % lon) ^ lon_mask)) for i in range(devices)]
        return lax.ppermute(data, AXES, pairs)

    dim = value.ndim - 2
    half = value.shape[dim] // 2
    core = lax.axis_index("lat") % 2
    kept = lax.dynamic_slice_in_dim(value, core * half, half, dim)
    sent = lax.dynamic_slice_in_dim(value, (1 - core) * half, half, dim)
    part = kept + send(sent, 1, 0)
    for bit in range(1, lat.bit_length() - 1):
        part = part + send(part, 1 << bit, 0)
    for bit in range(lon.bit_length() - 1):
        part = part + send(part, 0, (1 << (bit + 1)) - 1)
    other = send(part, 1, 0)
    low = jnp.where(core == 0, part, other)
    high = jnp.where(core == 0, other, part)
    return jnp.concatenate([low, high], axis=dim)


def shards(loadings):
    lat_rows, lon_cols, modes = loadings.shape
    lat_total = lat_rows * lax.axis_size("lat")
    lon_total = lon_cols * lax.axis_size("lon")
    count = group_of(lat_rows)
    steps = lat_rows // count
    pad = -(-lon_cols // 8) * 8
    tall = -(-modes // 16) * 16
    own_rows = lax.axis_index("lat") * lat_rows + jnp.arange(lat_rows)
    weights = latitude_weight(own_rows, lat_total)
    weight_lanes = jnp.repeat(weights, pad).reshape(steps, 1, count * pad)
    total = (jnp.sum(latitude_weight(jnp.arange(lat_total), lat_total)) * lon_total).reshape(1)
    stage = pltpu.VMEM((count * pad, modes), F32)
    vmem = pl.BlockSpec(memory_space=pltpu.VMEM)
    smem = pl.BlockSpec(memory_space=pltpu.SMEM)
    hbm = pl.BlockSpec(memory_space=pl.ANY)
    square = jax.ShapeDtypeStruct((modes, modes), F32)

    sums = pl.pallas_call(
        functools.partial(first_kernel, count=count),
        grid=(steps,),
        in_specs=[
            pl.BlockSpec((count, lon_cols, modes), lambda i: (i, 0, 0)),
            pl.BlockSpec((1, 1, count * pad), lambda i: (i, 0, 0)),
        ],
        out_specs=pl.BlockSpec((2, tall, modes), lambda i: (0, 0, 0)),
        out_shape=jax.ShapeDtypeStruct((2, tall, modes), F32),
        scratch_shapes=[stage],
        name="first_products",
    )(loadings, weight_lanes)
    sums = exchange_sum(sums)

    cubic, rotation = pl.pallas_call(
        functools.partial(middle_kernel, count=count),
        in_specs=[smem, vmem, vmem, hbm],
        out_specs=[vmem, vmem],
        out_shape=[jax.ShapeDtypeStruct((tall, modes), F32), square],
        scratch_shapes=[pltpu.VMEM(loadings.shape, F32), stage, pltpu.SemaphoreType.DMA(())],
        name="polar_and_products",
    )(total, sums, weight_lanes, loadings)
    cubic = exchange_sum(cubic)

    rotated, rotation = pl.pallas_call(
        last_kernel,
        in_specs=[smem, vmem, vmem, vmem, hbm],
        out_specs=[hbm, vmem],
        out_shape=[jax.ShapeDtypeStruct(loadings.shape, F32), square],
        scratch_shapes=[
            pltpu.VMEM(loadings.shape, F32),
            pltpu.VMEM(loadings.shape, F32),
            pltpu.SemaphoreType.DMA(()),
            pltpu.SemaphoreType.DMA((lat_rows,)),
        ],
        name="polar_and_rotate",
    )(total, sums, rotation, cubic, loadings)
    return (rotated, rotation)


def solution(mesh):
    return jax.shard_map(
        shards,
        mesh=mesh,
        in_specs=(P("lat", "lon", None),),
        out_specs=(P("lat", "lon", None), P()),
        check_vma=False,
    )
```

time: 407 us -> 108 us (0.27); the launches traced: 400 us -> 108 us
  waiting for transfers between devices: 212 us -> 36 us
  blocking collectives: 83.5 us -> 0 us
  matrix products: 71.6 us -> 0 us
  Pallas kernels: 0 us -> 43.8 us
  starting transfers between devices: 0.08 us -> 19.8 us
  between operations: 17.2 us -> 1.38 us
  local copies, waits for them, and re-layouts: 9.12 us -> 2.65 us
    psum x2 -> x0, waiting for transfers between devices: 212 us -> none  [reduce_pair(): return lax.psum((cubic, colsq), ('lat', 'lon'))]
    psum x2 -> x0, blocking collectives: 83.5 us -> none  [reduce_pair(): return lax.psum((cubic, colsq), ('lat', 'lon'))]
    dot_general x88 -> x0, matrix products: 71.6 us -> none  [matmul(): return jnp.dot(left, right, precision=lax.Precision.HIGHEST)]
    pallas_call x0 -> x3, Pallas kernels: none -> 43.8 us  [the longest x1 19.7 us: shards(): pl.pallas_call(functools.partial(middle_kernel, count=count), in_specs=[s...]
    ppermute x0 -> x12, waiting for transfers between devices: none -> 36 us  [send(): return lax.ppermute(data, AXES, pairs)]
    ppermute x0 -> x12, starting transfers between devices: none -> 19.8 us  [send(): return lax.ppermute(data, AXES, pairs)]
    reshape x2 -> x0, local copies, waits for them, and re-layouts: 8.73 us -> none  [shards(): normed = (loadings / row_norm).reshape(lat_rows * lon_cols, modes)]
  transfers between devices with their start and end apart: 2 -> 12, of which waited for: 2 -> 12; matrix products, arithmetic and copies ran while one was open for 0% -> 1% of each run, Pallas kernels for 0% -> 0%
where the time goes in v1:
time: 108 us
  Pallas kernels  43.8 us (41%)
  waiting for transfers between devices  36 us (33%)
  starting transfers between devices  19.8 us (18%)
  other arithmetic  4.27 us (4%)
  local copies, waits for them, and re-layouts  2.65 us (2%)
  between operations  1.38 us (1%)
    ppermute x12, waiting for transfers between devices, send(): return lax.ppermute(data, AXES, pairs)  36 us
    ppermute x12, starting transfers between devices, send(): return lax.ppermute(data, AXES, pairs)  19.8 us
    pallas_call x1, Pallas kernels, shards(): pl.pallas_call(functools.partial(middle_kernel, count=count), in_specs=[s...  19.7 us
    pallas_call x1, Pallas kernels, shards(): pl.pallas_call(last_kernel, in_specs=[smem, vmem, vmem, vmem, hbm], out_s...  17.2 us
    pallas_call x1, Pallas kernels, shards(): pl.pallas_call(functools.partial(first_kernel, count=count), grid=(steps,...  6.94 us
  transfers between devices with their start and end apart: 12, of which 12 were waited for; matrix products, arithmetic and copies ran while one was open for 1% of the time, Pallas kernels for 0%

profile of v1, /device:TPU:0, one launch (start us, length us, event | category | flops | bytes accessed | tf_op | source)
XLA Modules:
  0.0 107.9 jit_solution(18308124162463495917)
XLA Ops:
  0.6 0.1 multiply_cosine_fusion
  0.7 0.1 broadcast_in_dim.5
  0.8 0.7 broadcast_in_dim.7.w_ref
  1.5 6.9 %first_products.1 = f32[2,208,200]{2,1,0:T(8,128)} custom-call(f32[22,180,200]{2,1,0:T(8,128)} %x_hbm.3, f32[2,1,2024]{2,1,0:T(1,128)} %broadcast_in_dim.7.w_ref), custom_call_target="tpu_custom_call" | custom-call | tf_op jit(solution)/shard_map/first_products/pallas_call | solution.py:180
  8.4 0.9 constant_dynamic-slice_fusion.1
  9.4 0.6 collective-permute-start
  9.9 1.1 %collective-permute-done = f32[2,104,200]{2,1,0:T(8,128)S(1)} collective-permute-done((f32[2,104,200]{2,1,0:T(8,128)S(1)}, f32[2,104,200]{2,1,0:T(8,128)S(1)}, u32[]{:S(2)}, u32[]{:S(2)}) %collective-permute-start) | collective-permute-done | bytes 166432 | tf_op jit(solution)/shard_map/ppermute | solution.py:144
  11.0 1.0 dynamic-slice_add_fusion
  12.0 2.9 %collective-permute-start.1 = (f32[2,104,200]{2,1,0:T(8,128)S(1)}, f32[2,104,200]{2,1,0:T(8,128)S(1)}, u32[]{:S(2)}, u32[]{:S(2)}) collective-permute-start(f32[2,104,200]{2,1,0:T(8,128)S(1)} %dynamic-slice_add_fusion), channel_id=1, source_target_pairs={{0,8},{1,9},{2,10},{3,11},{4,12},{5,13},{6,14},{7,15},{8,0},{9,1},... | collective-permute-start | bytes 499208 | tf_op jit(solution)/shard_map/ppermute | solution.py:144
  14.9 5.6 %collective-permute-done.1 = f32[2,104,200]{2,1,0:T(8,128)S(1)} collective-permute-done((f32[2,104,200]{2,1,0:T(8,128)S(1)}, f32[2,104,200]{2,1,0:T(8,128)S(1)}, u32[]{:S(2)}, u32[]{:S(2)}) %collective-permute-start.1) | collective-permute-done | bytes 166432 | tf_op jit(solution)/shard_map/ppermute | solution.py:144
  20.5 1.8 %collective-permute-start.2 = (f32[2,104,200]{2,1,0:T(8,128)S(1)}, f32[2,104,200]{2,1,0:T(8,128)S(1)}, u32[]{:S(2)}, u32[]{:S(2)}) collective-permute-start(f32[2,104,200]{2,1,0:T(8,128)S(1)} %add.83), channel_id=1, source_target_pairs={{0,16},{1,17},{2,18},{3,19},{4,20},{5,21},{6,22},{7,23},{8,24},{9,... | collective-permute-start | bytes 499208 | tf_op jit(solution)/shard_map/ppermute | solution.py:144
  22.3 5.0 %collective-permute-done.2 = f32[2,104,200]{2,1,0:T(8,128)S(1)} collective-permute-done((f32[2,104,200]{2,1,0:T(8,128)S(1)}, f32[2,104,200]{2,1,0:T(8,128)S(1)}, u32[]{:S(2)}, u32[]{:S(2)}) %collective-permute-start.2) | collective-permute-done | bytes 166432 | tf_op jit(solution)/shard_map/ppermute | solution.py:144
  27.3 1.6 %collective-permute-start.3 = (f32[2,104,200]{2,1,0:T(8,128)S(1)}, f32[2,104,200]{2,1,0:T(8,128)S(1)}, u32[]{:S(2)}, u32[]{:S(2)}) collective-permute-start(f32[2,104,200]{2,1,0:T(8,128)S(1)} %add.84), channel_id=1, source_target_pairs={{0,1},{1,0},{2,3},{3,2},{4,5},{5,4},{6,7},{7,6},{8,9},{9,8},{10,11... | collective-permute-start | bytes 499208 | tf_op jit(solution)/shard_map/ppermute | solution.py:144
  28.9 4.3 %collective-permute-done.3 = f32[2,104,200]{2,1,0:T(8,128)S(1)} collective-permute-done((f32[2,104,200]{2,1,0:T(8,128)S(1)}, f32[2,104,200]{2,1,0:T(8,128)S(1)}, u32[]{:S(2)}, u32[]{:S(2)}) %collective-permute-start.3) | collective-permute-done | bytes 166432 | tf_op jit(solution)/shard_map/ppermute | solution.py:144
  33.3 3.6 %collective-permute-start.4 = (f32[2,104,200]{2,1,0:T(8,128)S(1)}, f32[2,104,200]{2,1,0:T(8,128)S(1)}, u32[]{:S(2)}, u32[]{:S(2)}) collective-permute-start(f32[2,104,200]{2,1,0:T(8,128)S(1)} %add.85), channel_id=1, source_target_pairs={{0,3},{1,2},{2,1},{3,0},{4,7},{5,6},{6,5},{7,4},{8,11},{9,10},{10,... | collective-permute-start | bytes 499208 | tf_op jit(solution)/shard_map/ppermute | solution.py:144
  36.9 4.2 %collective-permute-done.4 = f32[2,104,200]{2,1,0:T(8,128)S(1)} collective-permute-done((f32[2,104,200]{2,1,0:T(8,128)S(1)}, f32[2,104,200]{2,1,0:T(8,128)S(1)}, u32[]{:S(2)}, u32[]{:S(2)}) %collective-permute-start.4) | collective-permute-done | bytes 166432 | tf_op jit(solution)/shard_map/ppermute | solution.py:144
  41.1 0.1 collective-permute-start.5
  41.2 0.6 cosine_reduce_fusion
  42.5 0.1 collective-permute-done.5
  42.7 0.8 pad_maximum_fusion.sums_ref.gram_ref
  43.5 19.7 %polar_and_products.1 = (f32[208,200]{1,0:T(8,128)}, f32[200,200]{1,0:T(8,128)}) custom-call(f32[1]{0:T(128)} %bitcast.total_ref, f32[2,208,200]{2,1,0:T(8,128)} %pad_maximum_fusion.sums_ref.gram_ref, f32[2,1,2024]{2,1,0:T(1,128)} %broadcast_in_dim.7.w_ref, f32[22,180,200]{2,1,0:T(8,128)} %x_hbm.3), custom_call_target="tpu_custom_call" | custom-call | tf_op jit(solution)/shard_map/polar_and_products/pallas_call | solution.py:194
  63.2 0.9 constant_dynamic-slice_fusion
  64.1 0.4 collective-permute-start.6
  64.5 1.0 collective-permute-done.6
  65.4 0.9 dynamic-slice_add_fusion.1
  66.3 1.5 %collective-permute-start.7 = (f32[104,200]{1,0:T(8,128)S(1)}, f32[104,200]{1,0:T(8,128)S(1)}, u32[]{:S(2)}, u32[]{:S(2)}) collective-permute-start(f32[104,200]{1,0:T(8,128)S(1)} %dynamic-slice_add_fusion.1), channel_id=1, source_target_pairs={{0,8},{1,9},{2,10},{3,11},{4,12},{5,13},{6,14},{7,15},{8,0},{9,1},... | collective-permute-start | bytes 249608 | tf_op jit(solution)/shard_map/ppermute | solution.py:144
  67.8 3.8 %collective-permute-done.7 = f32[104,200]{1,0:T(8,128)S(1)} collective-permute-done((f32[104,200]{1,0:T(8,128)S(1)}, f32[104,200]{1,0:T(8,128)S(1)}, u32[]{:S(2)}, u32[]{:S(2)}) %collective-permute-start.7) | collective-permute-done | bytes 83232 | tf_op jit(solution)/shard_map/ppermute | solution.py:144
  71.7 1.5 %collective-permute-start.8 = (f32[104,200]{1,0:T(8,128)S(1)}, f32[104,200]{1,0:T(8,128)S(1)}, u32[]{:S(2)}, u32[]{:S(2)}) collective-permute-start(f32[104,200]{1,0:T(8,128)S(1)} %add.88), channel_id=1, source_target_pairs={{0,16},{1,17},{2,18},{3,19},{4,20},{5,21},{6,22},{7,23},{8,24},{9,... | collective-permute-start | bytes 249608 | tf_op jit(solution)/shard_map/ppermute | solution.py:144
  73.2 3.2 %collective-permute-done.8 = f32[104,200]{1,0:T(8,128)S(1)} collective-permute-done((f32[104,200]{1,0:T(8,128)S(1)}, f32[104,200]{1,0:T(8,128)S(1)}, u32[]{:S(2)}, u32[]{:S(2)}) %collective-permute-start.8) | collective-permute-done | bytes 83232 | tf_op jit(solution)/shard_map/ppermute | solution.py:144
  76.4 2.8 %collective-permute-start.9 = (f32[104,200]{1,0:T(8,128)S(1)}, f32[104,200]{1,0:T(8,128)S(1)}, u32[]{:S(2)}, u32[]{:S(2)}) collective-permute-start(f32[104,200]{1,0:T(8,128)S(1)} %add.89), channel_id=1, source_target_pairs={{0,1},{1,0},{2,3},{3,2},{4,5},{5,4},{6,7},{7,6},{8,9},{9,8},{10,11... | collective-permute-start | bytes 249608 | tf_op jit(solution)/shard_map/ppermute | solution.py:144
  79.3 2.7 %collective-permute-done.9 = f32[104,200]{1,0:T(8,128)S(1)} collective-permute-done((f32[104,200]{1,0:T(8,128)S(1)}, f32[104,200]{1,0:T(8,128)S(1)}, u32[]{:S(2)}, u32[]{:S(2)}) %collective-permute-start.9) | collective-permute-done | bytes 83232 | tf_op jit(solution)/shard_map/ppermute | solution.py:144
  82.0 2.9 %collective-permute-start.10 = (f32[104,200]{1,0:T(8,128)S(1)}, f32[104,200]{1,0:T(8,128)S(1)}, u32[]{:S(2)}, u32[]{:S(2)}) collective-permute-start(f32[104,200]{1,0:T(8,128)S(1)} %add.90), channel_id=1, source_target_pairs={{0,3},{1,2},{2,1},{3,0},{4,7},{5,6},{6,5},{7,4},{8,11},{9,10},{10,... | collective-permute-start | bytes 249608 | tf_op jit(solution)/shard_map/ppermute | solution.py:144
  84.8 3.8 %collective-permute-done.10 = f32[104,200]{1,0:T(8,128)S(1)} collective-permute-done((f32[104,200]{1,0:T(8,128)S(1)}, f32[104,200]{1,0:T(8,128)S(1)}, u32[]{:S(2)}, u32[]{:S(2)}) %collective-permute-start.10) | collective-permute-done | bytes 83232 | tf_op jit(solution)/shard_map/ppermute | solution.py:144
  88.7 0.1 collective-permute-start.11
  88.7 1.3 %collective-permute-done.11 = f32[104,200]{1,0:T(8,128)S(1)} collective-permute-done((f32[104,200]{1,0:T(8,128)S(1)}, f32[104,200]{1,0:T(8,128)S(1)}, u32[]{:S(2)}, u32[]{:S(2)}) %collective-permute-start.11) | collective-permute-done | bytes 83232 | tf_op jit(solution)/shard_map/ppermute | solution.py:144
  90.1 0.7 pad_maximum_fusion.1.cubic_ref
  90.8 17.2 %polar_and_rotate.1 = (f32[22,180,200]{2,1,0:T(8,128)}, f32[200,200]{1,0:T(8,128)}) custom-call(f32[1]{0:T(128)} %bitcast.total_ref, f32[2,208,200]{2,1,0:T(8,128)} %pad_maximum_fusion.sums_ref.gram_ref, f32[200,200]{1,0:T(8,128)} %get-tuple-element.4.old_ref, f32[208,200]{1,0:T(8,128)} %pad_maximum_fusion.1.cubic_ref, f32[22,180,200]{2,1,0:T(8,128)} %x_hbm.3), custom_call_target="tpu_custom_call" | custom-call | tf_op jit(solution)/shard_map/polar_and_rotate/pallas_call | solution.py:204
  (10 shorter events, 0.2 us)
Async XLA Ops:
  9.4 1.7 %collective-permute-start = (f32[2,104,200]{2,1,0:T(8,128)S(1)}, f32[2,104,200]{2,1,0:T(8,128)S(1)}, u32[]{:S(2)}, u32[]{:S(2)}) collective-permute-start(f32[2,104,200]{2,1,0:T(8,128)S(1)} %constant_dynamic-slice_fusion.1), channel_id=1, source_target_pairs={{0,4},{1,5},{2,6},{3,7},{4,0},{5,1},{6,2},{7,3},{8,12},{9,13},{10,... | collective-permute-start | bytes 499208 | tf_op jit(solution)/shard_map/ppermute | solution.py:144
  12.0 8.5 %collective-permute-start.1 = (f32[2,104,200]{2,1,0:T(8,128)S(1)}, f32[2,104,200]{2,1,0:T(8,128)S(1)}, u32[]{:S(2)}, u32[]{:S(2)}) collective-permute-start(f32[2,104,200]{2,1,0:T(8,128)S(1)} %dynamic-slice_add_fusion), channel_id=1, source_target_pairs={{0,8},{1,9},{2,10},{3,11},{4,12},{5,13},{6,14},{7,15},{8,0},{9,1},... | collective-permute-start | bytes 499208 | tf_op jit(solution)/shard_map/ppermute | solution.py:144
  20.5 6.8 %collective-permute-start.2 = (f32[2,104,200]{2,1,0:T(8,128)S(1)}, f32[2,104,200]{2,1,0:T(8,128)S(1)}, u32[]{:S(2)}, u32[]{:S(2)}) collective-permute-start(f32[2,104,200]{2,1,0:T(8,128)S(1)} %add.83), channel_id=1, source_target_pairs={{0,16},{1,17},{2,18},{3,19},{4,20},{5,21},{6,22},{7,23},{8,24},{9,... | collective-permute-start | bytes 499208 | tf_op jit(solution)/shard_map/ppermute | solution.py:144
  27.3 5.9 %collective-permute-start.3 = (f32[2,104,200]{2,1,0:T(8,128)S(1)}, f32[2,104,200]{2,1,0:T(8,128)S(1)}, u32[]{:S(2)}, u32[]{:S(2)}) collective-permute-start(f32[2,104,200]{2,1,0:T(8,128)S(1)} %add.84), channel_id=1, source_target_pairs={{0,1},{1,0},{2,3},{3,2},{4,5},{5,4},{6,7},{7,6},{8,9},{9,8},{10,11... | collective-permute-start | bytes 499208 | tf_op jit(solution)/shard_map/ppermute | solution.py:144
  33.3 7.8 %collective-permute-start.4 = (f32[2,104,200]{2,1,0:T(8,128)S(1)}, f32[2,104,200]{2,1,0:T(8,128)S(1)}, u32[]{:S(2)}, u32[]{:S(2)}) collective-permute-start(f32[2,104,200]{2,1,0:T(8,128)S(1)} %add.85), channel_id=1, source_target_pairs={{0,3},{1,2},{2,1},{3,0},{4,7},{5,6},{6,5},{7,4},{8,11},{9,10},{10,... | collective-permute-start | bytes 499208 | tf_op jit(solution)/shard_map/ppermute | solution.py:144
  41.1 1.5 %collective-permute-start.5 = (f32[2,104,200]{2,1,0:T(8,128)S(1)}, f32[2,104,200]{2,1,0:T(8,128)S(1)}, u32[]{:S(2)}, u32[]{:S(2)}) collective-permute-start(f32[2,104,200]{2,1,0:T(8,128)S(1)} %add.86), channel_id=1, source_target_pairs={{0,4},{1,5},{2,6},{3,7},{4,0},{5,1},{6,2},{7,3},{8,12},{9,13},{10,... | collective-permute-start | bytes 499208 | tf_op jit(solution)/shard_map/ppermute | solution.py:144
  64.1 1.3 %collective-permute-start.6 = (f32[104,200]{1,0:T(8,128)S(1)}, f32[104,200]{1,0:T(8,128)S(1)}, u32[]{:S(2)}, u32[]{:S(2)}) collective-permute-start(f32[104,200]{1,0:T(8,128)S(1)} %constant_dynamic-slice_fusion), channel_id=1, source_target_pairs={{0,4},{1,5},{2,6},{3,7},{4,0},{5,1},{6,2},{7,3},{8,12},{9,13},{10,... | collective-permute-start | bytes 249608 | tf_op jit(solution)/shard_map/ppermute | solution.py:144
  66.3 5.3 %collective-permute-start.7 = (f32[104,200]{1,0:T(8,128)S(1)}, f32[104,200]{1,0:T(8,128)S(1)}, u32[]{:S(2)}, u32[]{:S(2)}) collective-permute-start(f32[104,200]{1,0:T(8,128)S(1)} %dynamic-slice_add_fusion.1), channel_id=1, source_target_pairs={{0,8},{1,9},{2,10},{3,11},{4,12},{5,13},{6,14},{7,15},{8,0},{9,1},... | collective-permute-start | bytes 249608 | tf_op jit(solution)/shard_map/ppermute | solution.py:144
  71.7 4.8 %collective-permute-start.8 = (f32[104,200]{1,0:T(8,128)S(1)}, f32[104,200]{1,0:T(8,128)S(1)}, u32[]{:S(2)}, u32[]{:S(2)}) collective-permute-start(f32[104,200]{1,0:T(8,128)S(1)} %add.88), channel_id=1, source_target_pairs={{0,16},{1,17},{2,18},{3,19},{4,20},{5,21},{6,22},{7,23},{8,24},{9,... | collective-permute-start | bytes 249608 | tf_op jit(solution)/shard_map/ppermute | solution.py:144
  76.4 5.5 %collective-permute-start.9 = (f32[104,200]{1,0:T(8,128)S(1)}, f32[104,200]{1,0:T(8,128)S(1)}, u32[]{:S(2)}, u32[]{:S(2)}) collective-permute-start(f32[104,200]{1,0:T(8,128)S(1)} %add.89), channel_id=1, source_target_pairs={{0,1},{1,0},{2,3},{3,2},{4,5},{5,4},{6,7},{7,6},{8,9},{9,8},{10,11... | collective-permute-start | bytes 249608 | tf_op jit(solution)/shard_map/ppermute | solution.py:144
  82.0 6.7 %collective-permute-start.10 = (f32[104,200]{1,0:T(8,128)S(1)}, f32[104,200]{1,0:T(8,128)S(1)}, u32[]{:S(2)}, u32[]{:S(2)}) collective-permute-start(f32[104,200]{1,0:T(8,128)S(1)} %add.90), channel_id=1, source_target_pairs={{0,3},{1,2},{2,1},{3,0},{4,7},{5,6},{6,5},{7,4},{8,11},{9,10},{10,... | collective-permute-start | bytes 249608 | tf_op jit(solution)/shard_map/ppermute | solution.py:144
  88.7 1.4 %collective-permute-start.11 = (f32[104,200]{1,0:T(8,128)S(1)}, f32[104,200]{1,0:T(8,128)S(1)}, u32[]{:S(2)}, u32[]{:S(2)}) collective-permute-start(f32[104,200]{1,0:T(8,128)S(1)} %add.91), channel_id=1, source_target_pairs={{0,4},{1,5},{2,6},{3,7},{4,0},{5,1},{6,2},{7,3},{8,12},{9,13},{10,... | collective-permute-start | bytes 249608 | tf_op jit(solution)/shard_map/ppermute | solution.py:144

commit v2 on v1

v2 whole, which is shorter than its diff:
```python
import functools
import math

import jax
import jax.numpy as jnp
import numpy as np
from jax import lax
from jax.experimental import pallas as pl
from jax.experimental.pallas import tpu as pltpu
from jax.sharding import PartitionSpec as P

SWEEPS = 2
NS_STEPS = 20
AXES = ("lat", "lon")
F32 = jnp.float32
BF16 = jnp.bfloat16


def latitude_weight(rows, lat_total):
    degrees = -90.0 + (rows.astype(jnp.float32) + 0.5) * (180.0 / lat_total)
    return jnp.cos(degrees * (math.pi / 180.0))


def halves(value):
    high = value.astype(BF16)
    return high, (value - high.astype(F32)).astype(BF16)


def dot_nn(left, right):
    return lax.dot_general(left, right, (((1,), (0,)), ((), ())), preferred_element_type=F32)


def dot_nt(left, right):
    return lax.dot_general(left, right, (((1,), (1,)), ((), ())), preferred_element_type=F32)


def triple(dot, left, right):
    return dot(left[0], right[0]) + (dot(left[0], right[1]) + dot(left[1], right[0]))


def polar_transposed(gradient):
    iterate = gradient / jnp.sqrt(jnp.sum(gradient * gradient))

    def step(_, current):
        parts = halves(current)
        inner = triple(dot_nt, parts, parts)
        return 1.5 * current - 0.5 * triple(dot_nn, halves(inner), parts)

    return lax.fori_loop(0, NS_STEPS, step, iterate)


def group_of(lat_rows):
    return max(d for d in range(1, min(lat_rows, 11) + 1) if lat_rows % d == 0)


def normalize_rows(x_ref, first, count, stage):
    cols = x_ref.shape[1]
    pad = stage.shape[0] // count
    for r in range(count):
        x = x_ref[first + r]
        norm = jnp.sqrt(jnp.sum(x * x, axis=-1, keepdims=True) + 1e-06)
        stage[r * pad:r * pad + cols, :] = x * (1.0 / norm)


def products(left, parts):
    return triple(dot_nn, halves(left), parts)


def weight_lanes(w_ref, first, count, pad):
    lane = lax.broadcasted_iota(jnp.int32, (1, count * pad), 1)
    lanes = jnp.zeros((1, count * pad), F32)
    for r in range(count):
        lanes = jnp.where(lane >= r * pad, w_ref[first + r], lanes)
    return lanes


def half_of(ref, which):
    rows = ref.shape[0] // 2
    return ref.at[pl.ds(pl.multiple_of(which * rows, 8), rows), :]


def part_out(core_ref, sums_ref, kept_ref, sent_ref):
    kept_ref[...] = half_of(sums_ref, core_ref[0])[...]
    sent_ref[...] = half_of(sums_ref, 1 - core_ref[0])[...]


def put_together(core_ref, own_ref, other_ref, sums_ref):
    half_of(sums_ref, core_ref[0])[...] = own_ref[...]
    half_of(sums_ref, 1 - core_ref[0])[...] = other_ref[...]


def first_kernel(core_ref, w_ref, x_ref, kept_ref, sent_ref, stage, sums, *, count):
    step = pl.program_id(0)

    @pl.when(step == 0)
    def _():
        stage[...] = jnp.zeros_like(stage)
        sums[...] = jnp.zeros_like(sums)

    normalize_rows(x_ref, 0, count, stage)
    normed = stage[...]
    parts = halves(normed)
    flipped = normed.T
    weighted = flipped * weight_lanes(w_ref, step * count, count, stage.shape[0] // count)
    modes = normed.shape[1]
    tall = -(-modes // 8) * 8
    sums[0:modes, :] += products(weighted, parts)
    sums[tall:tall + modes, :] += products(weighted * flipped * flipped, parts)

    @pl.when(step == pl.num_programs(0) - 1)
    def _():
        part_out(core_ref, sums, kept_ref, sent_ref)


def diagonal(square):
    rows = lax.broadcasted_iota(jnp.int32, square.shape, 0)
    cols = lax.broadcasted_iota(jnp.int32, square.shape, 1)
    return jnp.sum(jnp.where(rows == cols, square, 0.0), axis=1, keepdims=True)


def middle_kernel(core_ref, w_ref, own_ref, other_ref, x_hbm, kept_ref, sent_ref, rot_ref, gram_ref,
                  x_ref, stage, sums, cubics, sem, *, count, total):
    copy = pltpu.make_async_copy(x_hbm, x_ref, sem)
    copy.start()
    modes = x_ref.shape[2]
    tall = -(-modes // 8) * 8
    put_together(core_ref, own_ref, other_ref, sums)
    gram = sums[0:modes, :]
    gram_ref[...] = gram
    rotation = polar_transposed(sums[tall:tall + modes, :] - gram * (diagonal(gram) / total))
    rot_ref[...] = rotation
    stage[...] = jnp.zeros_like(stage)
    cubics[...] = jnp.zeros_like(cubics)
    copy.wait()
    rot_parts = halves(rotation)

    def body(step, _):
        normalize_rows(x_ref, step * count, count, stage)
        parts = halves(stage[...])
        spun = triple(dot_nt, rot_parts, parts)
        lanes = weight_lanes(w_ref, step * count, count, stage.shape[0] // count)
        cubics[0:modes, :] += products(spun * spun * spun * lanes, parts)
        return 0

    lax.fori_loop(0, x_ref.shape[0] // count, body, 0)
    part_out(core_ref, cubics, kept_ref, sent_ref)


def last_kernel(core_ref, gram_ref, old_ref, own_ref, other_ref, x_hbm, out_hbm, rot_ref,
                x_ref, out_ref, cubics, sem, sems, *, total):
    copy = pltpu.make_async_copy(x_hbm, x_ref, sem)
    copy.start()
    lat_rows, _, modes = x_ref.shape
    put_together(core_ref, own_ref, other_ref, cubics)
    old = old_ref[...]
    turned = triple(dot_nn, halves(old), halves(gram_ref[...]))
    colsq = jnp.sum(turned * old, axis=1, keepdims=True)
    rotation = polar_transposed(cubics[0:modes, :] - turned * (colsq / total))
    rot_ref[...] = rotation.T
    parts = halves(rotation)
    copy.wait()
    writes = []
    for r in range(lat_rows):
        out_ref[r] = triple(dot_nt, halves(x_ref[r]), parts)
        write = pltpu.make_async_copy(out_ref.at[r], out_hbm.at[r], sems.at[r])
        write.start()
        writes.append(write)
    for write in writes:
        write.wait()


def tree_sum(values):
    while len(values) > 1:
        values = [left + right for left, right in zip(values[::2], values[1::2])]
    return values[0]


def exchange_sum(kept, sent):
    lon = lax.axis_size("lon")
    lat = lax.axis_size("lat")
    devices = lat * lon
    plane = lat // 2
    place = lax.axis_index("lat") // 2
    rows = kept.shape[0] // plane

    def send(data, lat_mask, lon_mask):
        pairs = [(i, ((i // lon) ^ lat_mask) * lon + ((i % lon) ^ lon_mask)) for i in range(devices)]
        return lax.ppermute(data, AXES, pairs)

    part = (kept + send(sent, 1, 0)).reshape(plane, rows, kept.shape[1])

    def chunk(array, mask):
        return lax.dynamic_index_in_dim(array, place ^ mask, 0, keepdims=False)

    own = tree_sum([chunk(part, 0)] + [send(chunk(part, m), 2 * m, 0) for m in range(1, plane)])
    own = tree_sum([own] + [send(own, 0, m) for m in range(1, lon)])
    gathered = jnp.stack([own] + [send(own, 2 * m, 0) for m in range(1, plane)])
    half = jnp.concatenate([chunk(gathered, m) for m in range(plane)])
    return half, send(half, 1, 0)


def shards(loadings):
    lat_rows, lon_cols, modes = loadings.shape
    lat = lax.axis_size("lat")
    lat_total = lat_rows * lat
    lon_total = lon_cols * lax.axis_size("lon")
    count = group_of(lat_rows)
    pad = -(-lon_cols // 8) * 8
    tall = -(-modes // 8) * 8
    own_rows = lax.axis_index("lat") * lat_rows + jnp.arange(lat_rows)
    weights = latitude_weight(own_rows, lat_total)
    degrees = -90.0 + (np.arange(lat_total) + 0.5) * (180.0 / lat_total)
    total = float(np.sum(np.cos(degrees * (math.pi / 180.0)))) * lon_total
    core = (lax.axis_index("lat") % 2).astype(jnp.int32).reshape(1)
    stage = pltpu.VMEM((count * pad, modes), F32)
    whole = pltpu.VMEM(loadings.shape, F32)
    vmem = pl.BlockSpec(memory_space=pltpu.VMEM)
    smem = pl.BlockSpec(memory_space=pltpu.SMEM)
    hbm = pl.BlockSpec(memory_space=pl.ANY)
    square = jax.ShapeDtypeStruct((modes, modes), F32)

    def half_rows(needed):
        return lat // 2 * (-(-needed // (8 * lat)) * 8)

    two, one = half_rows(2 * tall), half_rows(tall)
    half_two = jax.ShapeDtypeStruct((two, modes), F32)
    half_one = jax.ShapeDtypeStruct((one, modes), F32)
    sums = pltpu.VMEM((2 * two, modes), F32)
    cubics = pltpu.VMEM((2 * one, modes), F32)

    kept, sent = pl.pallas_call(
        functools.partial(first_kernel, count=count),
        grid=(lat_rows // count,),
        in_specs=[smem, smem, pl.BlockSpec((count, lon_cols, modes), lambda i: (i, 0, 0))],
        out_specs=[pl.BlockSpec((two, modes), lambda i: (0, 0))] * 2,
        out_shape=[half_two, half_two],
        scratch_shapes=[stage, sums],
        name="first_products",
    )(core, weights, loadings)
    own, other = exchange_sum(kept, sent)

    kept, sent, rotation, gram = pl.pallas_call(
        functools.partial(middle_kernel, count=count, total=total),
        in_specs=[smem, smem, vmem, vmem, hbm],
        out_specs=[vmem] * 4,
        out_shape=[half_one, half_one, square, square],
        scratch_shapes=[whole, stage, sums, cubics, pltpu.SemaphoreType.DMA(())],
        name="polar_and_products",
    )(core, weights, own, other, loadings)
    own, other = exchange_sum(kept, sent)

    rotated, rotation = pl.pallas_call(
        functools.partial(last_kernel, total=total),
        in_specs=[smem, vmem, vmem, vmem, vmem, hbm],
        out_specs=[hbm, vmem],
        out_shape=[jax.ShapeDtypeStruct(loadings.shape, F32), square],
        scratch_shapes=[whole, whole, cubics, pltpu.SemaphoreType.DMA(()), pltpu.SemaphoreType.DMA((lat_rows,))],
        name="polar_and_rotate",
    )(core, gram, rotation, own, other, loadings)
    return (rotated, rotation)


def solution(mesh):
    return jax.shard_map(
        shards,
        mesh=mesh,
        in_specs=(P("lat", "lon", None),),
        out_specs=(P("lat", "lon", None), P()),
        check_vma=False,
    )
```

time: 108 us -> 99.4 us (0.920)
  waiting for transfers between devices: 36 us -> 25.4 us
  starting transfers between devices: 19.8 us -> 24.9 us
  other arithmetic: 4.27 us -> 2.58 us
  local copies, waits for them, and re-layouts: 2.65 us -> 1.44 us
    ppermute x12 -> x22, waiting for transfers between devices: 36 us -> 25.4 us  [send(): return lax.ppermute(data, AXES, pairs)]
    ppermute x12 -> x22, starting transfers between devices: 19.8 us -> 24.9 us  [send(): return lax.ppermute(data, AXES, pairs)]
    dynamic_slice x2 -> x0, local copies, waits for them, and re-layouts: 1.86 us -> none  [exchange_sum(): sent = lax.dynamic_slice_in_dim(value, (1 - core) * half, half, dim)]
    concatenate x2, other arithmetic: 1.48 us -> 0.04 us  [exchange_sum(): half = jnp.concatenate([chunk(gathered, m) for m in range(plane)])]
    unnamed x0 -> x8, local copies, waits for them, and re-layouts: none -> 1.35 us
  transfers between devices with their start and end apart: 12 -> 22, of which waited for: 12 -> 21; matrix products, arithmetic and copies ran while one was open for 1% -> 0% of each run, Pallas kernels for 0% -> 0%
where the time goes in v2:
time: 99.4 us; the launch traced here: 99.2 us
  Pallas kernels  44.1 us (44%)
  waiting for transfers between devices  25.4 us (26%)
  starting transfers between devices  24.9 us (25%)
  other arithmetic  2.58 us (3%)
  local copies, waits for them, and re-layouts  1.44 us (1%)
    ppermute x22, waiting for transfers between devices, send(): return lax.ppermute(data, AXES, pairs)  25.4 us
    ppermute x22, starting transfers between devices, send(): return lax.ppermute(data, AXES, pairs)  24.9 us
    pallas_call x1, Pallas kernels, shards(): pl.pallas_call(functools.partial(middle_kernel, count=count, total=total)...  19.9 us
    pallas_call x1, Pallas kernels, shards(): pl.pallas_call(functools.partial(last_kernel, total=total), in_specs=[sme...  17.2 us
    pallas_call x1, Pallas kernels, shards(): pl.pallas_call(functools.partial(first_kernel, count=count), grid=(lat_ro...  7.02 us
  transfers between devices with their start and end apart: 22, of which 21 were waited for; matrix products, arithmetic and copies ran while one was open for 0% of the time, Pallas kernels for 0%

profile of v2, /device:TPU:0, one launch (start us, length us, event | category | flops | bytes accessed | tf_op | source)
XLA Modules:
  0.0 99.2 jit_solution(5874889318289767381)
XLA Ops:
  0.6 0.6 multiply_cosine_fusion.w_ref
  1.2 7.0 %first_products.1 = (f32[224,200]{1,0:T(8,128)}, f32[224,200]{1,0:T(8,128)}) custom-call(s32[1]{0:T(128)} %bitcast.core_ref, f32[22]{0:T(128)} %multiply_cosine_fusion.w_ref, f32[22,180,200]{2,1,0:T(8,128)} %x_hbm.3), custom_call_target="tpu_custom_call" | custom-call | tf_op jit(solution)/shard_map/first_products/pallas_call | solution.py:231
  8.2 0.5 collective-permute-start
  8.7 1.3 %collective-permute-done = f32[224,200]{1,0:T(8,128)S(1)} collective-permute-done((f32[224,200]{1,0:T(8,128)}, f32[224,200]{1,0:T(8,128)S(1)}, u32[]{:S(2)}, u32[]{:S(2)}) %collective-permute-start) | collective-permute-done | bytes 179232 | tf_op jit(solution)/shard_map/ppermute | solution.py:188
  10.0 1.0 add.90
  11.1 3.9 %collective-permute-start.3 = (f32[56,200]{1,0:T(8,128)S(1)}, f32[56,200]{1,0:T(8,128)S(1)}, u32[]{:S(2)}, u32[]{:S(2)}) collective-permute-start(f32[56,200]{1,0:T(8,128)S(1)} %get-tuple-element.18), channel_id=1, source_target_pairs={{0,24},{1,25},{2,26},{3,27},{4,28},{5,29},{6,30},{7,31},{8,16},{9,... | collective-permute-start | bytes 134408 | tf_op jit(solution)/shard_map/ppermute | solution.py:188
  14.9 0.5 collective-permute-start.2
  15.4 0.1 collective-permute-start.1
  15.6 1.6 %collective-permute-done.3 = f32[56,200]{1,0:T(8,128)S(1)} collective-permute-done((f32[56,200]{1,0:T(8,128)S(1)}, f32[56,200]{1,0:T(8,128)S(1)}, u32[]{:S(2)}, u32[]{:S(2)}) %collective-permute-start.3) | collective-permute-done | bytes 44832 | tf_op jit(solution)/shard_map/ppermute | solution.py:188
  17.1 2.0 %collective-permute-done.2 = f32[56,200]{1,0:T(8,128)S(1)} collective-permute-done((f32[56,200]{1,0:T(8,128)S(1)}, f32[56,200]{1,0:T(8,128)S(1)}, u32[]{:S(2)}, u32[]{:S(2)}) %collective-permute-start.2) | collective-permute-done | bytes 44832 | tf_op jit(solution)/shard_map/ppermute | solution.py:188
  19.1 0.5 collective-permute-done.1
  19.6 3.7 %collective-permute-start.6 = (f32[56,200]{1,0:T(8,128)S(1)}, f32[56,200]{1,0:T(8,128)S(1)}, u32[]{:S(2)}, u32[]{:S(2)}) collective-permute-start(f32[56,200]{1,0:T(8,128)S(1)} %fusion), channel_id=1, source_target_pairs={{0,3},{1,2},{2,1},{3,0},{4,7},{5,6},{6,5},{7,4},{8,11},{9,10},{10,... | collective-permute-start | bytes 134408 | tf_op jit(solution)/shard_map/ppermute | solution.py:188
  23.3 0.0 collective-permute-start.5
  23.3 0.8 collective-permute-start.4
  24.1 1.7 %collective-permute-done.6 = f32[56,200]{1,0:T(8,128)S(1)} collective-permute-done((f32[56,200]{1,0:T(8,128)S(1)}, f32[56,200]{1,0:T(8,128)S(1)}, u32[]{:S(2)}, u32[]{:S(2)}) %collective-permute-start.6) | collective-permute-done | bytes 44832 | tf_op jit(solution)/shard_map/ppermute | solution.py:188
  25.8 2.6 %collective-permute-done.5 = f32[56,200]{1,0:T(8,128)S(1)} collective-permute-done((f32[56,200]{1,0:T(8,128)S(1)}, f32[56,200]{1,0:T(8,128)S(1)}, u32[]{:S(2)}, u32[]{:S(2)}) %collective-permute-start.5) | collective-permute-done | bytes 44832 | tf_op jit(solution)/shard_map/ppermute | solution.py:188
  28.4 0.0 collective-permute-done.4
  28.4 1.6 %collective-permute-start.9 = (f32[56,200]{1,0:T(8,128)S(1)}, f32[56,200]{1,0:T(8,128)S(1)}, u32[]{:S(2)}, u32[]{:S(2)}) collective-permute-start(f32[56,200]{1,0:T(8,128)S(1)} %add_add_fusion), channel_id=1, source_target_pairs={{0,24},{1,25},{2,26},{3,27},{4,28},{5,29},{6,30},{7,31},{8,16},{9,... | collective-permute-start | bytes 134408 | tf_op jit(solution)/shard_map/ppermute | solution.py:188
  29.9 0.5 collective-permute-start.8
  30.5 1.5 %collective-permute-start.7 = (f32[56,200]{1,0:T(8,128)S(1)}, f32[56,200]{1,0:T(8,128)S(1)}, u32[]{:S(2)}, u32[]{:S(2)}) collective-permute-start(f32[56,200]{1,0:T(8,128)S(1)} %add_add_fusion), channel_id=1, source_target_pairs={{0,8},{1,9},{2,10},{3,11},{4,12},{5,13},{6,14},{7,15},{8,0},{9,1},... | collective-permute-start | bytes 134408 | tf_op jit(solution)/shard_map/ppermute | solution.py:188
  31.9 1.6 %collective-permute-done.9 = f32[56,200]{1,0:T(8,128)S(1)} collective-permute-done((f32[56,200]{1,0:T(8,128)S(1)}, f32[56,200]{1,0:T(8,128)S(1)}, u32[]{:S(2)}, u32[]{:S(2)}) %collective-permute-start.9) | collective-permute-done | bytes 44832 | tf_op jit(solution)/shard_map/ppermute | solution.py:188
  33.5 0.6 collective-permute-done.8
  34.1 0.5 collective-permute-done.7
  34.7 0.0 copy-start
  34.7 0.1 collective-permute-start.10
  34.8 1.5 %collective-permute-done.10.other_ref = f32[224,200]{1,0:T(8,128)S(1)} collective-permute-done((f32[224,200]{1,0:T(8,128)S(1)}, f32[224,200]{1,0:T(8,128)S(1)}, u32[]{:S(2)}, u32[]{:S(2)}) %collective-permute-start.10) | collective-permute-done | bytes 179232 | tf_op jit(solution)/shard_map/ppermute | solution.py:188
  36.3 0.0 copy-done
  36.3 0.0 copy-start.2
  36.3 0.7 copy-done.2
  37.0 19.9 %polar_and_products.1 = (f32[128,200]{1,0:T(8,128)}, f32[128,200]{1,0:T(8,128)}, f32[200,200]{1,0:T(8,128)}, f32[200,200]{1,0:T(8,128)}) custom-call(s32[1]{0:T(128)} %bitcast.core_ref, f32[22]{0:T(128)} %multiply_cosine_fusion.w_ref, f32[224,200]{1,0:T(8,128)} %copy-done, f32[224,200]{1,0:T(8,128)} %copy-done.2, f32[22,180,200]{2,1,0:T(8,128)} %x_hbm.3), custom_call_target="tpu_custom_call" | custom-call | tf_op jit(solution)/shard_map/polar_and_products/pallas_call | solution.py:242
  56.9 0.2 collective-permute-start.11
  57.1 1.4 %collective-permute-done.11 = f32[128,200]{1,0:T(8,128)S(1)} collective-permute-done((f32[128,200]{1,0:T(8,128)}, f32[128,200]{1,0:T(8,128)S(1)}, u32[]{:S(2)}, u32[]{:S(2)}) %collective-permute-start.11) | collective-permute-done | bytes 102432 | tf_op jit(solution)/shard_map/ppermute | solution.py:188
  58.5 0.9 add.101
  59.4 2.5 %collective-permute-start.14 = (f32[32,200]{1,0:T(8,128)S(1)}, f32[32,200]{1,0:T(8,128)S(1)}, u32[]{:S(2)}, u32[]{:S(2)}) collective-permute-start(f32[32,200]{1,0:T(8,128)S(1)} %get-tuple-element.25), channel_id=1, source_target_pairs={{0,24},{1,25},{2,26},{3,27},{4,28},{5,29},{6,30},{7,31},{8,16},{9,... | collective-permute-start | bytes 76808 | tf_op jit(solution)/shard_map/ppermute | solution.py:188
  62.0 0.5 collective-permute-start.13
  62.5 0.5 collective-permute-start.12
  63.0 1.3 %collective-permute-done.14 = f32[32,200]{1,0:T(8,128)S(1)} collective-permute-done((f32[32,200]{1,0:T(8,128)S(1)}, f32[32,200]{1,0:T(8,128)S(1)}, u32[]{:S(2)}, u32[]{:S(2)}) %collective-permute-start.14) | collective-permute-done | bytes 25632 | tf_op jit(solution)/shard_map/ppermute | solution.py:188
  64.3 1.6 %collective-permute-done.13 = f32[32,200]{1,0:T(8,128)S(1)} collective-permute-done((f32[32,200]{1,0:T(8,128)S(1)}, f32[32,200]{1,0:T(8,128)S(1)}, u32[]{:S(2)}, u32[]{:S(2)}) %collective-permute-start.13) | collective-permute-done | bytes 25632 | tf_op jit(solution)/shard_map/ppermute | solution.py:188
  65.9 0.5 collective-permute-done.12
  66.4 1.6 %collective-permute-start.17 = (f32[32,200]{1,0:T(8,128)S(1)}, f32[32,200]{1,0:T(8,128)S(1)}, u32[]{:S(2)}, u32[]{:S(2)}) collective-permute-start(f32[32,200]{1,0:T(8,128)S(1)} %fusion.1), channel_id=1, source_target_pairs={{0,3},{1,2},{2,1},{3,0},{4,7},{5,6},{6,5},{7,4},{8,11},{9,10},{10,... | collective-permute-start | bytes 76808 | tf_op jit(solution)/shard_map/ppermute | solution.py:188
  68.0 0.6 collective-permute-start.16
  68.6 2.3 %collective-permute-start.15 = (f32[32,200]{1,0:T(8,128)S(1)}, f32[32,200]{1,0:T(8,128)S(1)}, u32[]{:S(2)}, u32[]{:S(2)}) collective-permute-start(f32[32,200]{1,0:T(8,128)S(1)} %fusion.1), channel_id=1, source_target_pairs={{0,1},{1,0},{2,3},{3,2},{4,5},{5,4},{6,7},{7,6},{8,9},{9,8},{10,11... | collective-permute-start | bytes 76808 | tf_op jit(solution)/shard_map/ppermute | solution.py:188
  70.8 1.3 %collective-permute-done.17 = f32[32,200]{1,0:T(8,128)S(1)} collective-permute-done((f32[32,200]{1,0:T(8,128)S(1)}, f32[32,200]{1,0:T(8,128)S(1)}, u32[]{:S(2)}, u32[]{:S(2)}) %collective-permute-start.17) | collective-permute-done | bytes 25632 | tf_op jit(solution)/shard_map/ppermute | solution.py:188
  72.2 0.7 collective-permute-done.16
  72.9 0.2 collective-permute-done.15
  73.1 1.6 %collective-permute-start.20 = (f32[32,200]{1,0:T(8,128)S(1)}, f32[32,200]{1,0:T(8,128)S(1)}, u32[]{:S(2)}, u32[]{:S(2)}) collective-permute-start(f32[32,200]{1,0:T(8,128)S(1)} %add_add_fusion.1), channel_id=1, source_target_pairs={{0,24},{1,25},{2,26},{3,27},{4,28},{5,29},{6,30},{7,31},{8,16},{9,... | collective-permute-start | bytes 76808 | tf_op jit(solution)/shard_map/ppermute | solution.py:188
  74.7 1.3 %collective-permute-start.19 = (f32[32,200]{1,0:T(8,128)S(1)}, f32[32,200]{1,0:T(8,128)S(1)}, u32[]{:S(2)}, u32[]{:S(2)}) collective-permute-start(f32[32,200]{1,0:T(8,128)S(1)} %add_add_fusion.1), channel_id=1, source_target_pairs={{0,16},{1,17},{2,18},{3,19},{4,20},{5,21},{6,22},{7,23},{8,24},{9,... | collective-permute-start | bytes 76808 | tf_op jit(solution)/shard_map/ppermute | solution.py:188
  76.0 0.7 collective-permute-start.18
  76.7 1.3 %collective-permute-done.20 = f32[32,200]{1,0:T(8,128)S(1)} collective-permute-done((f32[32,200]{1,0:T(8,128)S(1)}, f32[32,200]{1,0:T(8,128)S(1)}, u32[]{:S(2)}, u32[]{:S(2)}) %collective-permute-start.20) | collective-permute-done | bytes 25632 | tf_op jit(solution)/shard_map/ppermute | solution.py:188
  78.0 0.6 collective-permute-done.19
  78.6 1.3 %collective-permute-done.18 = f32[32,200]{1,0:T(8,128)S(1)} collective-permute-done((f32[32,200]{1,0:T(8,128)S(1)}, f32[32,200]{1,0:T(8,128)S(1)}, u32[]{:S(2)}, u32[]{:S(2)}) %collective-permute-start.18) | collective-permute-done | bytes 25632 | tf_op jit(solution)/shard_map/ppermute | solution.py:188
  79.9 0.0 copy-start.1
  79.9 0.1 collective-permute-start.21
  80.0 1.3 %collective-permute-done.21.other_ref = f32[128,200]{1,0:T(8,128)S(1)} collective-permute-done((f32[128,200]{1,0:T(8,128)S(1)}, f32[128,200]{1,0:T(8,128)S(1)}, u32[]{:S(2)}, u32[]{:S(2)}) %collective-permute-start.21) | collective-permute-done | bytes 102432 | tf_op jit(solution)/shard_map/ppermute | solution.py:188
  81.4 0.0 copy-start.3
  81.4 0.0 copy-done.1
  81.4 0.6 copy-done.3
  82.0 17.2 %polar_and_rotate.1 = (f32[22,180,200]{2,1,0:T(8,128)}, f32[200,200]{1,0:T(8,128)}) custom-call(s32[1]{0:T(128)} %bitcast.core_ref, f32[200,200]{1,0:T(8,128)} %get-tuple-element.10.gram_ref, f32[200,200]{1,0:T(8,128)} %get-tuple-element.11.old_ref, f32[128,200]{1,0:T(8,128)} %copy-done.1, f32[128,200]{1,0:T(8,128)} %copy-done.3, f32[22,180,200]{2,1,0:T(8,128)} %x_hbm.3), custom_call_target="tpu_custom_call" | custom-call | tf_op jit(solution)/shard_map/polar_and_rotate/pallas_call | solution.py:252
  (12 shorter events, 0.2 us)
Async XLA Ops:
  8.2 1.8 %collective-permute-start = (f32[224,200]{1,0:T(8,128)}, f32[224,200]{1,0:T(8,128)S(1)}, u32[]{:S(2)}, u32[]{:S(2)}) collective-permute-start(f32[224,200]{1,0:T(8,128)} %get-tuple-element.9), channel_id=1, source_target_pairs={{0,4},{1,5},{2,6},{3,7},{4,0},{5,1},{6,2},{7,3},{8,12},{9,13},{10,... | collective-permute-start | bytes 537608 | tf_op jit(solution)/shard_map/ppermute | solution.py:188
  11.1 6.1 %collective-permute-start.3 = (f32[56,200]{1,0:T(8,128)S(1)}, f32[56,200]{1,0:T(8,128)S(1)}, u32[]{:S(2)}, u32[]{:S(2)}) collective-permute-start(f32[56,200]{1,0:T(8,128)S(1)} %get-tuple-element.18), channel_id=1, source_target_pairs={{0,24},{1,25},{2,26},{3,27},{4,28},{5,29},{6,30},{7,31},{8,16},{9,... | collective-permute-start | bytes 134408 | tf_op jit(solution)/shard_map/ppermute | solution.py:188
  14.9 4.2 %collective-permute-start.2 = (f32[56,200]{1,0:T(8,128)S(1)}, f32[56,200]{1,0:T(8,128)S(1)}, u32[]{:S(2)}, u32[]{:S(2)}) collective-permute-start(f32[56,200]{1,0:T(8,128)S(1)} %get-tuple-element.19), channel_id=1, source_target_pairs={{0,16},{1,17},{2,18},{3,19},{4,20},{5,21},{6,22},{7,23},{8,24},{9,... | collective-permute-start | bytes 134408 | tf_op jit(solution)/shard_map/ppermute | solution.py:188
  15.4 4.2 %collective-permute-start.1 = (f32[56,200]{1,0:T(8,128)S(1)}, f32[56,200]{1,0:T(8,128)S(1)}, u32[]{:S(2)}, u32[]{:S(2)}) collective-permute-start(f32[56,200]{1,0:T(8,128)S(1)} %get-tuple-element.20), channel_id=1, source_target_pairs={{0,8},{1,9},{2,10},{3,11},{4,12},{5,13},{6,14},{7,15},{8,0},{9,1},... | collective-permute-start | bytes 134408 | tf_op jit(solution)/shard_map/ppermute | solution.py:188
  19.6 6.1 %collective-permute-start.6 = (f32[56,200]{1,0:T(8,128)S(1)}, f32[56,200]{1,0:T(8,128)S(1)}, u32[]{:S(2)}, u32[]{:S(2)}) collective-permute-start(f32[56,200]{1,0:T(8,128)S(1)} %fusion), channel_id=1, source_target_pairs={{0,3},{1,2},{2,1},{3,0},{4,7},{5,6},{6,5},{7,4},{8,11},{9,10},{10,... | collective-permute-start | bytes 134408 | tf_op jit(solution)/shard_map/ppermute | solution.py:188
  23.3 5.1 %collective-permute-start.5 = (f32[56,200]{1,0:T(8,128)S(1)}, f32[56,200]{1,0:T(8,128)S(1)}, u32[]{:S(2)}, u32[]{:S(2)}) collective-permute-start(f32[56,200]{1,0:T(8,128)S(1)} %fusion), channel_id=1, source_target_pairs={{0,2},{1,3},{2,0},{3,1},{4,6},{5,7},{6,4},{7,5},{8,10},{9,11},{10,... | collective-permute-start | bytes 134408 | tf_op jit(solution)/shard_map/ppermute | solution.py:188
  23.3 5.1 %collective-permute-start.4 = (f32[56,200]{1,0:T(8,128)S(1)}, f32[56,200]{1,0:T(8,128)S(1)}, u32[]{:S(2)}, u32[]{:S(2)}) collective-permute-start(f32[56,200]{1,0:T(8,128)S(1)} %fusion), channel_id=1, source_target_pairs={{0,1},{1,0},{2,3},{3,2},{4,5},{5,4},{6,7},{7,6},{8,9},{9,8},{10,11... | collective-permute-start | bytes 134408 | tf_op jit(solution)/shard_map/ppermute | solution.py:188
  28.4 5.1 %collective-permute-start.9 = (f32[56,200]{1,0:T(8,128)S(1)}, f32[56,200]{1,0:T(8,128)S(1)}, u32[]{:S(2)}, u32[]{:S(2)}) collective-permute-start(f32[56,200]{1,0:T(8,128)S(1)} %add_add_fusion), channel_id=1, source_target_pairs={{0,24},{1,25},{2,26},{3,27},{4,28},{5,29},{6,30},{7,31},{8,16},{9,... | collective-permute-start | bytes 134408 | tf_op jit(solution)/shard_map/ppermute | solution.py:188
  29.9 4.2 %collective-permute-start.8 = (f32[56,200]{1,0:T(8,128)S(1)}, f32[56,200]{1,0:T(8,128)S(1)}, u32[]{:S(2)}, u32[]{:S(2)}) collective-permute-start(f32[56,200]{1,0:T(8,128)S(1)} %add_add_fusion), channel_id=1, source_target_pairs={{0,16},{1,17},{2,18},{3,19},{4,20},{5,21},{6,22},{7,23},{8,24},{9,... | collective-permute-start | bytes 134408 | tf_op jit(solution)/shard_map/ppermute | solution.py:188
  30.5 4.2 %collective-permute-start.7 = (f32[56,200]{1,0:T(8,128)S(1)}, f32[56,200]{1,0:T(8,128)S(1)}, u32[]{:S(2)}, u32[]{:S(2)}) collective-permute-start(f32[56,200]{1,0:T(8,128)S(1)} %add_add_fusion), channel_id=1, source_target_pairs={{0,8},{1,9},{2,10},{3,11},{4,12},{5,13},{6,14},{7,15},{8,0},{9,1},... | collective-permute-start | bytes 134408 | tf_op jit(solution)/shard_map/ppermute | solution.py:188
  34.7 1.6 %copy-start = (f32[224,200]{1,0:T(8,128)}, f32[224,200]{1,0:T(8,128)S(1)}, u32[]{:S(2)}) copy-start(f32[224,200]{1,0:T(8,128)S(1)} %pad_maximum_fusion.1.own_ref) | copy-start | bytes 537604
  34.7 1.6 %collective-permute-start.10 = (f32[224,200]{1,0:T(8,128)S(1)}, f32[224,200]{1,0:T(8,128)S(1)}, u32[]{:S(2)}, u32[]{:S(2)}) collective-permute-start(f32[224,200]{1,0:T(8,128)S(1)} %pad_maximum_fusion.1.own_ref), channel_id=1, source_target_pairs={{0,4},{1,5},{2,6},{3,7},{4,0},{5,1},{6,2},{7,3},{8,12},{9,13},{10,... | collective-permute-start | bytes 537608 | tf_op jit(solution)/shard_map/ppermute | solution.py:188
  36.3 0.7 copy-start.2
  56.9 1.6 %collective-permute-start.11 = (f32[128,200]{1,0:T(8,128)}, f32[128,200]{1,0:T(8,128)S(1)}, u32[]{:S(2)}, u32[]{:S(2)}) collective-permute-start(f32[128,200]{1,0:T(8,128)} %get-tuple-element.13), channel_id=1, source_target_pairs={{0,4},{1,5},{2,6},{3,7},{4,0},{5,1},{6,2},{7,3},{8,12},{9,13},{10,... | collective-permute-start | bytes 307208 | tf_op jit(solution)/shard_map/ppermute | solution.py:188
  59.4 4.9 %collective-permute-start.14 = (f32[32,200]{1,0:T(8,128)S(1)}, f32[32,200]{1,0:T(8,128)S(1)}, u32[]{:S(2)}, u32[]{:S(2)}) collective-permute-start(f32[32,200]{1,0:T(8,128)S(1)} %get-tuple-element.25), channel_id=1, source_target_pairs={{0,24},{1,25},{2,26},{3,27},{4,28},{5,29},{6,30},{7,31},{8,16},{9,... | collective-permute-start | bytes 76808 | tf_op jit(solution)/shard_map/ppermute | solution.py:188
  62.0 3.9 %collective-permute-start.13 = (f32[32,200]{1,0:T(8,128)S(1)}, f32[32,200]{1,0:T(8,128)S(1)}, u32[]{:S(2)}, u32[]{:S(2)}) collective-permute-start(f32[32,200]{1,0:T(8,128)S(1)} %get-tuple-element.26), channel_id=1, source_target_pairs={{0,16},{1,17},{2,18},{3,19},{4,20},{5,21},{6,22},{7,23},{8,24},{9,... | collective-permute-start | bytes 76808 | tf_op jit(solution)/shard_map/ppermute | solution.py:188
  62.5 3.9 %collective-permute-start.12 = (f32[32,200]{1,0:T(8,128)S(1)}, f32[32,200]{1,0:T(8,128)S(1)}, u32[]{:S(2)}, u32[]{:S(2)}) collective-permute-start(f32[32,200]{1,0:T(8,128)S(1)} %get-tuple-element.27), channel_id=1, source_target_pairs={{0,8},{1,9},{2,10},{3,11},{4,12},{5,13},{6,14},{7,15},{8,0},{9,1},... | collective-permute-start | bytes 76808 | tf_op jit(solution)/shard_map/ppermute | solution.py:188
  66.4 5.8 %collective-permute-start.17 = (f32[32,200]{1,0:T(8,128)S(1)}, f32[32,200]{1,0:T(8,128)S(1)}, u32[]{:S(2)}, u32[]{:S(2)}) collective-permute-start(f32[32,200]{1,0:T(8,128)S(1)} %fusion.1), channel_id=1, source_target_pairs={{0,3},{1,2},{2,1},{3,0},{4,7},{5,6},{6,5},{7,4},{8,11},{9,10},{10,... | collective-permute-start | bytes 76808 | tf_op jit(solution)/shard_map/ppermute | solution.py:188
  68.0 4.9 %collective-permute-start.16 = (f32[32,200]{1,0:T(8,128)S(1)}, f32[32,200]{1,0:T(8,128)S(1)}, u32[]{:S(2)}, u32[]{:S(2)}) collective-permute-start(f32[32,200]{1,0:T(8,128)S(1)} %fusion.1), channel_id=1, source_target_pairs={{0,2},{1,3},{2,0},{3,1},{4,6},{5,7},{6,4},{7,5},{8,10},{9,11},{10,... | collective-permute-start | bytes 76808 | tf_op jit(solution)/shard_map/ppermute | solution.py:188
  68.6 4.5 %collective-permute-start.15 = (f32[32,200]{1,0:T(8,128)S(1)}, f32[32,200]{1,0:T(8,128)S(1)}, u32[]{:S(2)}, u32[]{:S(2)}) collective-permute-start(f32[32,200]{1,0:T(8,128)S(1)} %fusion.1), channel_id=1, source_target_pairs={{0,1},{1,0},{2,3},{3,2},{4,5},{5,4},{6,7},{7,6},{8,9},{9,8},{10,11... | collective-permute-start | bytes 76808 | tf_op jit(solution)/shard_map/ppermute | solution.py:188
  73.1 4.9 %collective-permute-start.20 = (f32[32,200]{1,0:T(8,128)S(1)}, f32[32,200]{1,0:T(8,128)S(1)}, u32[]{:S(2)}, u32[]{:S(2)}) collective-permute-start(f32[32,200]{1,0:T(8,128)S(1)} %add_add_fusion.1), channel_id=1, source_target_pairs={{0,24},{1,25},{2,26},{3,27},{4,28},{5,29},{6,30},{7,31},{8,16},{9,... | collective-permute-start | bytes 76808 | tf_op jit(solution)/shard_map/ppermute | solution.py:188
  74.7 3.9 %collective-permute-start.19 = (f32[32,200]{1,0:T(8,128)S(1)}, f32[32,200]{1,0:T(8,128)S(1)}, u32[]{:S(2)}, u32[]{:S(2)}) collective-permute-start(f32[32,200]{1,0:T(8,128)S(1)} %add_add_fusion.1), channel_id=1, source_target_pairs={{0,16},{1,17},{2,18},{3,19},{4,20},{5,21},{6,22},{7,23},{8,24},{9,... | collective-permute-start | bytes 76808 | tf_op jit(solution)/shard_map/ppermute | solution.py:188
  76.0 3.9 %collective-permute-start.18 = (f32[32,200]{1,0:T(8,128)S(1)}, f32[32,200]{1,0:T(8,128)S(1)}, u32[]{:S(2)}, u32[]{:S(2)}) collective-permute-start(f32[32,200]{1,0:T(8,128)S(1)} %add_add_fusion.1), channel_id=1, source_target_pairs={{0,8},{1,9},{2,10},{3,11},{4,12},{5,13},{6,14},{7,15},{8,0},{9,1},... | collective-permute-start | bytes 76808 | tf_op jit(solution)/shard_map/ppermute | solution.py:188
  79.9 1.4 %copy-start.1 = (f32[128,200]{1,0:T(8,128)}, f32[128,200]{1,0:T(8,128)S(1)}, u32[]{:S(2)}) copy-start(f32[128,200]{1,0:T(8,128)S(1)} %pad_maximum_fusion.3.own_ref) | copy-start | bytes 307204
  79.9 1.4 %collective-permute-start.21 = (f32[128,200]{1,0:T(8,128)S(1)}, f32[128,200]{1,0:T(8,128)S(1)}, u32[]{:S(2)}, u32[]{:S(2)}) collective-permute-start(f32[128,200]{1,0:T(8,128)S(1)} %pad_maximum_fusion.3.own_ref), channel_id=1, source_target_pairs={{0,4},{1,5},{2,6},{3,7},{4,0},{5,1},{6,2},{7,3},{8,12},{9,13},{10,... | collective-permute-start | bytes 307208 | tf_op jit(solution)/shard_map/ppermute | solution.py:188
  81.4 0.7 copy-start.3
